TPU v7x, 512 devices: a whole 4x8x8 slice. The times are simulated.
512 devices in a mesh: seq: 32 (over z_hi, y, core), mp: 16 (over z_lo, x).
Axes of the slice: x: 4, y: 8, z: 8 (z_hi: 2, z_lo: 4; z = z_hi * 4 + z_lo), core: 2. Of those that a mesh axis runs over, the one named last changes fastest.
Arguments:
- inputs: bfloat16 [32768, 4096], P('seq', 'mp'), may hold values from -6 to 6
- conv_weight: bfloat16 [4, 4096], P(None, 'mp'), may hold values from -3 to 3
- conv_bias: bfloat16 [4096], P('mp'), may hold values from -3 to 3
- doc_start: int32 [32768], P('seq'), may hold values from 0 to 32767, as said below
- counts: int32 [32], P('seq'), may hold values from 341 to 1024
Outputs:
- gram: float32 [4096, 4096], P('seq', 'mp')
Inputs may be any that keep to these rules, and one draw needn't show every extreme that they name: doc_start is never above the token's own position, and for t > 0 either doc_start[t] == t or doc_start[t] == doc_start[t - 1]; doc_start[0] is 0.
All inputs are finite; a program needn't handle non-finite values.
Results may differ from a plain program's by a relative error of at most 0.0003.
Values may be sent and summed in bfloat16 or wider, within the bound.
No kernel may reach another device: no remote copies, remote signals or barrier semaphores. Data moves between devices by JAX's collectives and lax.ppermute only.
A program may use at most 64 MiB of HBM per device.

v0:
```python
import jax
import jax.numpy as jnp
from jax import lax
from jax.sharding import Mesh
from jax.sharding import PartitionSpec as P

SEQ = ("seq_0", "seq_1", "seq_2")


def sent_to_all(x, axis):
    copies = jnp.broadcast_to(x, (lax.axis_size(axis), *x.shape))
    return lax.all_to_all(copies, axis, split_axis=0, concat_axis=0, tiled=True)


def taken_together(x, axis):
    everything = sent_to_all(x, axis)
    return jnp.sum(everything, axis=0)


def passed_along(x, axis, by):
    peers = lax.axis_size(axis)
    pairs = [(i, i + by) for i in range(peers) if 0 <= i + by < peers]
    return lax.ppermute(x, axis, pairs)


def cut_along(x, dim, peers):
    dims = x.shape
    pieces = x.reshape(*dims[:dim], peers, dims[dim] // peers, *dims[dim + 1 :])
    return jnp.moveaxis(pieces, dim, 0)


def summed_on_arrival(x, axis, dim):
    pieces = cut_along(x, dim, lax.axis_size(axis))
    arrived = lax.all_to_all(pieces, axis, split_axis=0, concat_axis=0, tiled=True)
    return arrived.sum(axis=0)


def sum_in_two_steps(x, axes, dim):
    far, near = axes
    pieces = cut_along(x, dim, lax.axis_size(far))
    nearer = summed_on_arrival(pieces, near, dim + 1)
    arrived = lax.all_to_all(nearer, far, split_axis=0, concat_axis=0, tiled=True)
    return arrived.sum(axis=0)


def causal_conv(extended, weights, bias, position, doc_start, length):
    kernel_len = weights.shape[0]
    summed = jnp.zeros((length, weights.shape[1]), jnp.float32) + bias.astype(jnp.float32)
    for lag in range(kernel_len):
        window = extended[kernel_len - 1 - lag : kernel_len - 1 - lag + length].astype(jnp.float32)
        usable = position - lag >= doc_start
        summed = summed + jnp.where(usable[:, None], weights[lag].astype(jnp.float32) * window, 0.0)
    return jax.nn.silu(summed).astype(jnp.bfloat16)


def on_device(inputs, conv_weight, conv_bias, doc_start, counts):
    row_count = inputs.shape[0]
    kernel_len = conv_weight.shape[0]
    position = lax.axis_index(SEQ) * row_count + jnp.arange(row_count, dtype=jnp.int32)
    counted = jnp.arange(row_count, dtype=jnp.int32) < counts[0]
    token_total = taken_together(counts.astype(jnp.float32)[0], SEQ)
    prior = passed_along(inputs[row_count - (kernel_len - 1) :], SEQ, 1)
    extended = jnp.concatenate([prior, inputs], axis=0)
    own_feats = causal_conv(extended, conv_weight, conv_bias, position, doc_start, row_count)
    kept = jnp.where(counted[:, None], own_feats, jnp.zeros_like(own_feats))
    whole = lax.all_gather(own_feats, "mp", axis=1, tiled=True)
    summed = sum_in_two_steps(
        lax.dot_general(whole, kept, (((0,), (0,)), ((), ())), preferred_element_type=jnp.float32),
        (("seq_0", "seq_1"), "seq_2"),
        0,
    )
    return summed / token_total


def solution(mesh):
    torus = Mesh(mesh.devices.reshape(2, 8, 2, mesh.shape["mp"]), ("seq_0", "seq_1", "seq_2", "mp"))
    placed = (P(SEQ, "mp"), P(None, "mp"), P("mp"), P(SEQ), P(SEQ))
    return jax.shard_map(
        on_device, mesh=torus, in_specs=placed, out_specs=P(SEQ, "mp"), check_vma=False
    )
```

profile of v0, /device:TPU:33, one launch (start us, length us, event | category | flops | bytes accessed | tf_op | source)
XLA Modules:
  0.0 267.8 jit_solution(6630288082526933012)
XLA Ops:
  6.5 0.0 all-gather.2.cloned.1.call-start
  6.5 0.7 slice.26
  7.2 2.9 %collective-permute-start = (bf16[3,256]{1,0:T(4,128)(2,1)S(1)}, bf16[3,256]{1,0:T(4,128)(2,1)S(1)}, u32[]{:S(2)}, u32[]{:S(2)}) collective-permute-start(bf16[3,256]{1,0:T(4,128)(2,1)S(1)} %slice.26), channel_id=1, source_target_pairs={{0,16},{16,32},{32,48},{48,64},{64,80},{80,96},{96,112},{112,128},... | collective-permute-start | bytes 4616 | tf_op jit(solution)/shard_map/ppermute | solution.py:23
  10.1 0.7 fusion.6
  10.8 0.8 slice_convert_fusion.3
  11.6 0.7 convert_element_type.29
  12.3 0.0 collective-permute-done
  12.3 4.5 %multiply_convert_fusion = bf16[1024,256]{1,0:T(8,128)(2,1)} fusion(bf16[1024,256]{1,0:T(8,128)(2,1)} %param.5, bf16[3,256]{1,0:T(4,128)(2,1)S(1)} %collective-permute-done, f32[256]{0:T(256)S(1)} %bitcast.16, f32[256]{0:T(256)S(1)} %bitcast.17, f32[256]{0:T(256)S(1)} %bitcast.15, f32[256]{0:T(256)S(1)} %bitcast.14, f32[256]{0:T(256)S(1)} %convert_element_type.29, ...), kind=kLoop, calls=%fused_computation.1 | loop fusion | flops 7864320 | bytes 1059328 | tf_op jit(solution)/shard_map/convert_element_type | solution.py:53
  16.8 0.0 all-gather.2.cloned.1.call-update
  17.5 121.6 %all-gather.2.cloned.1.call-done = bf16[1024,4096]{1,0:T(8,128)(2,1)} async-done(((bf16[1024,256]{1,0:T(8,128)(2,1)}), bf16[1024,4096]{1,0:T(8,128)(2,1)}) %all-gather.2.cloned.1.call-update) | async-done | bytes 8388624 | tf_op jit(solution)/shard_map/all_gather | solution.py:66
  139.0 6.0 %fusion.2 = f32[4096,256]{1,0:T(8,128)S(1)} fusion(bf16[1024,4096]{1,0:T(8,128)(2,1)} %all-gather.2.cloned.1.call-done, bf16[1024,256]{1,0:T(8,128)(2,1)} %multiply_convert_fusion, pred[1024]{0:T(1024)(128)(4,1)S(1)} %iota_compare_fusion), kind=kOutput, calls=%fused_computation.7 | convolution fusion | flops 2147745792 | bytes 13108224 | tf_op jit(solution)/shard_map/dot_general | solution.py:68
  145.0 0.4 copy.12
  145.5 17.4 %all_to_all.16 = f32[2,16,128,256]{3,2,1,0:T(8,128)} all-to-all(f32[2,16,128,256]{3,2,1,0:T(8,128)S(1)} %bitcast.12), channel_id=1, replica_groups=mesh['seq_0'=2,'seq_1'=8,'seq_2'=2,'mp'=16] {'seq_2'}, dimensions={0} | all-to-all | bytes 8388608 | tf_op jit(solution)/shard_map/all_to_all | solution.py:34
  162.9 0.6 broadcast_in_dim.61
  163.5 11.9 %all-to-all-start.2 = ((f32[32,1,1]{2,1,0:T(1,128)}), f32[32,1,1]{2,1,0:T(1,128)S(1)}, u32[]{:S(2)}, u32[]{:S(2)}) async-start(f32[32,1,1]{2,1,0:T(1,128)} %broadcast_in_dim.61), calls=%async_computation.2 | async-start | bytes 32768 | tf_op jit(solution)/shard_map/all_to_all | solution.py:12
  175.4 4.0 %reduce_sum.27 = f32[16,128,256]{2,1,0:T(8,128)} reduce(f32[2,16,128,256]{3,2,1,0:T(8,128)} %all_to_all.16, f32[]{:T(128)} %constant.32.clone.1), dimensions={0}, to_apply=%region_0.0 | reduce | flops 524288 | bytes 6291460 | tf_op jit(solution)/shard_map/reduce_sum | solution.py:35
  179.5 2.8 %all-to-all-done.2 = f32[32,1,1]{2,1,0:T(1,128)S(1)} async-done(((f32[32,1,1]{2,1,0:T(1,128)}), f32[32,1,1]{2,1,0:T(1,128)S(1)}, u32[]{:S(2)}, u32[]{:S(2)}) %all-to-all-start.2) | async-done | bytes 160 | tf_op jit(solution)/shard_map/all_to_all | solution.py:12
  182.2 8.7 %all-to-all-start.1 = ((f32[16,128,256]{2,1,0:T(8,128)}), f32[16,128,256]{2,1,0:T(8,128)S(1)}, u32[]{:S(2)}, u32[]{:S(2)}) async-start(f32[16,128,256]{2,1,0:T(8,128)} %reduce_sum.27), calls=%async_computation.1 | async-start | bytes 4194304 | tf_op jit(solution)/shard_map/all_to_all | solution.py:42
  191.0 0.7 reduce_sum.29
  191.6 67.9 %all-to-all-done.1 = f32[16,128,256]{2,1,0:T(8,128)S(1)} async-done(((f32[16,128,256]{2,1,0:T(8,128)}), f32[16,128,256]{2,1,0:T(8,128)S(1)}, u32[]{:S(2)}, u32[]{:S(2)}) %all-to-all-start.1) | async-done | bytes 2097184 | tf_op jit(solution)/shard_map/all_to_all | solution.py:42
  259.6 0.1 reduce_sum.28
  259.7 1.3 broadcast_divide_fusion
  (1 shorter events, 0.0 us)
Async XLA Ops:
  6.5 132.5 %all-gather.2.cloned.1.call-start = ((), (), s32[]{:S(2)}) async-start(), calls=%async_computation.3 | async-start | bytes 8912896 | tf_op jit(solution)/shard_map/all_gather | solution.py:66
  7.2 5.1 %collective-permute-start = (bf16[3,256]{1,0:T(4,128)(2,1)S(1)}, bf16[3,256]{1,0:T(4,128)(2,1)S(1)}, u32[]{:S(2)}, u32[]{:S(2)}) collective-permute-start(bf16[3,256]{1,0:T(4,128)(2,1)S(1)} %slice.26), channel_id=1, source_target_pairs={{0,16},{16,32},{32,48},{48,64},{64,80},{80,96},{96,112},{112,128},... | collective-permute-start | bytes 4616 | tf_op jit(solution)/shard_map/ppermute | solution.py:23
  163.5 18.7 %all-to-all-start.2 = ((f32[32,1,1]{2,1,0:T(1,128)}), f32[32,1,1]{2,1,0:T(1,128)S(1)}, u32[]{:S(2)}, u32[]{:S(2)}) async-start(f32[32,1,1]{2,1,0:T(1,128)} %broadcast_in_dim.61), calls=%async_computation.2 | async-start | bytes 32768 | tf_op jit(solution)/shard_map/all_to_all | solution.py:12
  182.2 77.3 %all-to-all-start.1 = ((f32[16,128,256]{2,1,0:T(8,128)}), f32[16,128,256]{2,1,0:T(8,128)S(1)}, u32[]{:S(2)}, u32[]{:S(2)}) async-start(f32[16,128,256]{2,1,0:T(8,128)} %reduce_sum.27), calls=%async_computation.1 | async-start | bytes 4194304 | tf_op jit(solution)/shard_map/all_to_all | solution.py:42
Sparse Core Ops, SparseCore 0:
  16.9 122.0 all-gather.1
where the time goes:
time: 268 us
  waiting for transfers between devices  192 us (72%)
  starting transfers between devices  23.5 us (9%)
  blocking collectives  17.4 us (6%)
  between operations  14.1 us (5%)
  other arithmetic  12.8 us (5%)
  matrix products  5.99 us (2%)
    all_gather x1, waiting for transfers between devices, on_device(): whole = lax.all_gather(own_feats, 'mp', axis=1, tiled=True)  122 us
    all_to_all x1, waiting for transfers between devices, sum_in_two_steps(): lax.all_to_all(nearer, far, split_axis=0, concat_axis=0, tiled=True)  67.9 us
    all_to_all x1, blocking collectives, summed_on_arrival(): lax.all_to_all(pieces, axis, split_axis=0, concat_axis=0, tiled=True)  17.4 us
    all_to_all x1, starting transfers between devices, sent_to_all(): return lax.all_to_all(copies, axis, split_axis=0, concat_axis=0, tiled=True)  11.9 us
    all_to_all x1, starting transfers between devices, sum_in_two_steps(): lax.all_to_all(nearer, far, split_axis=0, concat_axis=0, tiled=True)  8.74 us
    dot_general x1, matrix products, on_device(): lax.dot_general(whole, kept, (((0,), (0,)), ((), ())), preferred_element_...  5.99 us
  transfers between devices with their start and end apart: 4, of which 3 were waited for; matrix products, arithmetic and copies ran while one was open for 3% of the time, Pallas kernels for 0%

commit v1 on v0

--- a/solution.py
+++ b/solution.py
@@ -1,3 +1,4 @@
+import functools
 import jax
 import jax.numpy as jnp
 from jax import lax
@@ -5,6 +6,16 @@
 from jax.sharding import PartitionSpec as P
 
 SEQ = ("seq_0", "seq_1", "seq_2")
+
+
+def save_samples(chunk, a_name):
+    after = jnp.stack([chunk for _ in range(jax.lax.axis_size(a_name))])
+    b_next = jax.lax.all_to_all(after, a_name, 0, 0)
+    h_now = jnp.concatenate(b_next, 1)
+    return h_now
+
+
+_draft_links = functools.partial(save_samples, a_name="mp")
 
 
 def sent_to_all(x, axis):
@@ -63,7 +74,7 @@
     extended = jnp.concatenate([prior, inputs], axis=0)
     own_feats = causal_conv(extended, conv_weight, conv_bias, position, doc_start, row_count)
     kept = jnp.where(counted[:, None], own_feats, jnp.zeros_like(own_feats))
-    whole = lax.all_gather(own_feats, "mp", axis=1, tiled=True)
+    whole = _draft_links(own_feats)
     summed = sum_in_two_steps(
         lax.dot_general(whole, kept, (((0,), (0,)), ((), ())), preferred_element_type=jnp.float32),
         (("seq_0", "seq_1"), "seq_2"),

time: 268 us -> 313 us (1.17)
  the two profiles are of different devices: /device:TPU:33 before, /device:TPU:92 now
where the time goes in v1:
time: 313 us
  waiting for transfers between devices  248 us (79%)
  starting transfers between devices  30.8 us (10%)
  other arithmetic  12.2 us (4%)
  blocking collectives  8.32 us (3%)
  local copies, waits for them, and re-layouts  6.24 us (2%)
  matrix products  5.84 us (2%)
    all_to_all x1, waiting for transfers between devices, save_samples(): b_next = jax.lax.all_to_all(after, a_name, 0, 0)  183 us
    all_to_all x1, waiting for transfers between devices, sum_in_two_steps(): lax.all_to_all(nearer, far, split_axis=0, concat_axis=0, tiled=True)  60 us
    all_to_all x1, starting transfers between devices, sent_to_all(): return lax.all_to_all(copies, axis, split_axis=0, concat_axis=0, tiled=True)  12.7 us
    all_to_all x1, starting transfers between devices, save_samples(): b_next = jax.lax.all_to_all(after, a_name, 0, 0)  9.34 us
    all_to_all x1, blocking collectives, summed_on_arrival(): lax.all_to_all(pieces, axis, split_axis=0, concat_axis=0, tiled=True)  8.32 us
    all_to_all x1, starting transfers between devices, sum_in_two_steps(): lax.all_to_all(nearer, far, split_axis=0, concat_axis=0, tiled=True)  6.9 us
  transfers between devices with their start and end apart: 4, of which 4 were waited for; matrix products, arithmetic and copies ran while one was open for 2% of the time, Pallas kernels for 0%

profile of v1, /device:TPU:92, one launch (start us, length us, event | category | flops | bytes accessed | tf_op | source)
XLA Modules:
  0.0 312.6 jit_solution(6863636739102600136)
XLA Ops:
  0.0 0.7 slice.26
  0.7 1.9 collective-permute-start
  2.6 0.7 fusion.6
  3.3 0.8 slice_convert_fusion.3
  4.2 0.7 convert_element_type.29
  4.8 0.8 collective-permute-done
  5.6 3.9 %multiply_convert_fusion = bf16[1024,256]{1,0:T(8,128)(2,1)S(1)} fusion(bf16[1024,256]{1,0:T(8,128)(2,1)} %param.5, bf16[3,256]{1,0:T(4,128)(2,1)S(1)} %collective-permute-done, f32[256]{0:T(256)S(1)} %bitcast.24, f32[256]{0:T(256)S(1)} %bitcast.25, f32[256]{0:T(256)S(1)} %bitcast.23, f32[256]{0:T(256)S(1)} %bitcast.22, f32[256]{0:T(256)S(1)} %convert_element_type.29, ...), kind=kLoop, calls=%fused_computation.1 | loop fusion | flops 7864320 | bytes 1059328 | tf_op jit(solution)/shard_map/convert_element_type | solution.py:64
  9.5 0.2 copy.11
  9.7 4.3 %stack.2 = bf16[16,1024,256]{1,2,0:T(8,128)(2,1)} broadcast(bf16[1024,256]{0,1:T(8,128)(2,1)S(1)} %copy.11), dimensions={1,2} | broadcast | bytes 8912896 | tf_op jit(solution)/shard_map/stack | solution.py:12
  14.0 9.3 %all-to-all-start = ((bf16[16,1024,256]{1,2,0:T(8,128)(2,1)}), bf16[16,1024,256]{1,2,0:T(8,128)(2,1)}, u32[]{:S(2)}, u32[]{:S(2)}) async-start(bf16[16,1024,256]{1,2,0:T(8,128)(2,1)} %stack.2), calls=%async_computation | async-start | bytes 16777216 | tf_op jit(solution)/shard_map/all_to_all | solution.py:13
  24.0 182.5 %all-to-all-done = bf16[16,1024,256]{1,2,0:T(8,128)(2,1)} async-done(((bf16[16,1024,256]{1,2,0:T(8,128)(2,1)}), bf16[16,1024,256]{1,2,0:T(8,128)(2,1)}, u32[]{:S(2)}, u32[]{:S(2)}) %all-to-all-start) | async-done | bytes 8388640 | tf_op jit(solution)/shard_map/all_to_all | solution.py:13
  206.5 5.8 %convolution_bitcast_fusion = f32[2,16,128,256]{3,2,0,1:T(8,128)S(1)} fusion(bf16[16,2,128,1024]{3,2,1,0:T(8,128)(2,1)} %bitcast.7, bf16[1024,256]{1,0:T(8,128)(2,1)S(1)} %multiply_convert_fusion, pred[1024]{0:T(1024)(128)(4,1)S(1)} %iota_compare_fusion), kind=kOutput, calls=%fused_computation | convolution fusion | flops 2147745792 | bytes 13108224 | tf_op jit(solution)/shard_map/dot_general | solution.py:79
  212.4 0.4 copy.12
  212.8 8.3 %all_to_all.21 = f32[2,16,128,256]{3,2,1,0:T(8,128)} all-to-all(f32[2,16,128,256]{3,2,1,0:T(8,128)S(1)} %copy.12), channel_id=1, replica_groups=mesh['seq_0'=2,'seq_1'=8,'seq_2'=2,'mp'=16] {'seq_2'}, dimensions={0} | all-to-all | bytes 8388608 | tf_op jit(solution)/shard_map/all_to_all | solution.py:45
  221.1 0.6 broadcast_in_dim.61
  221.8 12.7 %all-to-all-start.3 = ((f32[32,1,1]{2,1,0:T(1,128)}), f32[32,1,1]{2,1,0:T(1,128)S(1)}, u32[]{:S(2)}, u32[]{:S(2)}) async-start(f32[32,1,1]{2,1,0:T(1,128)} %broadcast_in_dim.61), calls=%async_computation.3 | async-start | bytes 32768 | tf_op jit(solution)/shard_map/all_to_all | solution.py:23
  234.4 4.1 %reduce_sum.27 = f32[16,128,256]{2,1,0:T(8,128)} reduce(f32[2,16,128,256]{3,2,1,0:T(8,128)} %all_to_all.21, f32[]{:T(128)} %constant.32.clone.1), dimensions={0}, to_apply=%region_0.0 | reduce | flops 524288 | bytes 6291460 | tf_op jit(solution)/shard_map/reduce_sum | solution.py:46
  238.5 5.2 %all-to-all-done.3 = f32[32,1,1]{2,1,0:T(1,128)S(1)} async-done(((f32[32,1,1]{2,1,0:T(1,128)}), f32[32,1,1]{2,1,0:T(1,128)S(1)}, u32[]{:S(2)}, u32[]{:S(2)}) %all-to-all-start.3) | async-done | bytes 160 | tf_op jit(solution)/shard_map/all_to_all | solution.py:23
  243.7 6.9 %all-to-all-start.2 = ((f32[16,128,256]{2,1,0:T(8,128)}), f32[16,128,256]{2,1,0:T(8,128)S(1)}, u32[]{:S(2)}, u32[]{:S(2)}) async-start(f32[16,128,256]{2,1,0:T(8,128)} %reduce_sum.27), calls=%async_computation.2 | async-start | bytes 4194304 | tf_op jit(solution)/shard_map/all_to_all | solution.py:53
  250.6 0.6 reduce_sum.29
  251.2 60.0 %all-to-all-done.2 = f32[16,128,256]{2,1,0:T(8,128)S(1)} async-done(((f32[16,128,256]{2,1,0:T(8,128)}), f32[16,128,256]{2,1,0:T(8,128)S(1)}, u32[]{:S(2)}, u32[]{:S(2)}) %all-to-all-start.2) | async-done | bytes 2097184 | tf_op jit(solution)/shard_map/all_to_all | solution.py:53
  311.2 0.1 reduce_sum.28
  311.4 1.2 broadcast_divide_fusion
  (1 shorter events, 0.0 us)
Async XLA Ops:
  0.7 4.9 %collective-permute-start = (bf16[3,256]{1,0:T(4,128)(2,1)S(1)}, bf16[3,256]{1,0:T(4,128)(2,1)S(1)}, u32[]{:S(2)}, u32[]{:S(2)}) collective-permute-start(bf16[3,256]{1,0:T(4,128)(2,1)S(1)} %slice.26), channel_id=1, source_target_pairs={{0,16},{16,32},{32,48},{48,64},{64,80},{80,96},{96,112},{112,128},... | collective-permute-start | bytes 4616 | tf_op jit(solution)/shard_map/ppermute | solution.py:34
  14.0 192.5 %all-to-all-start = ((bf16[16,1024,256]{1,2,0:T(8,128)(2,1)}), bf16[16,1024,256]{1,2,0:T(8,128)(2,1)}, u32[]{:S(2)}, u32[]{:S(2)}) async-start(bf16[16,1024,256]{1,2,0:T(8,128)(2,1)} %stack.2), calls=%async_computation | async-start | bytes 16777216 | tf_op jit(solution)/shard_map/all_to_all | solution.py:13
  221.8 21.9 %all-to-all-start.3 = ((f32[32,1,1]{2,1,0:T(1,128)}), f32[32,1,1]{2,1,0:T(1,128)S(1)}, u32[]{:S(2)}, u32[]{:S(2)}) async-start(f32[32,1,1]{2,1,0:T(1,128)} %broadcast_in_dim.61), calls=%async_computation.3 | async-start | bytes 32768 | tf_op jit(solution)/shard_map/all_to_all | solution.py:23
  243.7 67.6 %all-to-all-start.2 = ((f32[16,128,256]{2,1,0:T(8,128)}), f32[16,128,256]{2,1,0:T(8,128)S(1)}, u32[]{:S(2)}, u32[]{:S(2)}) async-start(f32[16,128,256]{2,1,0:T(8,128)} %reduce_sum.27), calls=%async_computation.2 | async-start | bytes 4194304 | tf_op jit(solution)/shard_map/all_to_all | solution.py:53
